TPU v7x, 128 devices: a whole 4x4x4 slice. The times are simulated.
128 devices in a mesh: pb: 16 (over z, y_hi, core), ka: 8 (over x, y_lo).
Axes of the slice: x: 4, y: 4 (y_hi: 2, y_lo: 2; y = y_hi * 2 + y_lo), z: 4, core: 2. Of those that a mesh axis runs over, the one named last changes fastest.
Arguments:
- activations: bfloat16 [4, 4096, 768], P(None, ('pb', 'ka')), may hold values from -6 to 6
- attn_gain: float32 [768], replicated, may hold values from 0.1 to 1.9
- w_qkv: bfloat16 [768, 2304], replicated, may hold values from -0.21875 to 0.21875
- w_gate: bfloat16 [768, 768], replicated, may hold values from -0.21875 to 0.21875
- w_out: bfloat16 [768, 768], replicated, may hold values from -0.21875 to 0.21875
- pair_bias: bfloat16 [16, 4096, 4096], P(None, 'pb', 'ka'), may hold values from -240 to 240
- chain_ids: int32 [4096], replicated, may hold values from 0 to 5, as said below
- binder_flag: int32 [4096], replicated, may hold values from 0 to 1, as said below
- trans_gain: float32 [768], replicated, may hold values from 0.1 to 1.9
- w_up: bfloat16 [768, 3072], replicated, may hold values from -0.21875 to 0.21875
- w_down: bfloat16 [1536, 768], replicated, may hold values from -0.15625 to 0.15625
Outputs:
- updated: bfloat16 [4, 4096, 768], P(None, ('pb', 'ka'))
Inputs may be any that keep to these rules, and one draw needn't show every extreme that they name: `chain_ids`: chain ids never fall along the tokens; every chain has at least one token. `binder_flag`: all tokens of one chain carry the same flag.
All inputs are finite; a program needn't handle non-finite values.
Results may differ from a plain program's by a relative error of at most 0.0056.
Values may be sent and summed in bfloat16 or wider, within the bound.
A program may use at most 128 MiB of HBM per device.

v0:
```python
import math

import jax
import jax.numpy as jnp
from jax import lax
from jax.sharding import PartitionSpec as P

epsilon = 1e-05
masked_score = -1000000000.0


def in_one_piece(arrays, axis, dim, along):
    ends, at = ([], 0)
    for a in arrays[:-1]:
        at += a.shape[along]
        ends.append(at)
    both = jnp.concatenate(arrays, axis=along)
    return tuple(jnp.split(lax.all_gather(both, axis, axis=dim, tiled=True), ends, axis=along))


def spread_2(value, axis, source):
    kept = jnp.where(lax.axis_index(axis) == source, value, 0).astype(value.dtype)
    return lax.psum(kept, axis)


def layer_norm(values, scales):
    centred = values - jnp.mean(values, axis=-1, keepdims=True)
    spread = jnp.mean(centred * centred, axis=-1, keepdims=True)
    return centred * lax.rsqrt(spread + epsilon) * scales


def block_stats(query_rows, key_block, value_block, bias_tile, allowed):
    head_count = bias_tile.shape[0]
    query_heads = query_rows.reshape(query_rows.shape[0], head_count, -1)
    key_heads = key_block.reshape(key_block.shape[0], head_count, -1)
    value_heads = value_block.reshape(value_block.shape[0], head_count, -1)
    head_size = query_heads.shape[-1]
    scores = jnp.einsum(
        "qhd,khd->hqk", query_heads, key_heads, preferred_element_type=jnp.float32
    ) / math.sqrt(head_size)
    scores = scores + bias_tile.astype(jnp.float32)
    best_score = jnp.max(jnp.where(allowed[None], scores, masked_score), axis=-1)
    weights = jnp.where(allowed[None], jnp.exp(scores - best_score[..., None]), 0.0)
    row_sum = jnp.sum(weights, axis=-1)
    block_out = jnp.einsum(
        "hqk,khd->qhd",
        weights.astype(jnp.bfloat16),
        value_heads,
        preferred_element_type=jnp.float32,
    )
    return (best_score.T, row_sum.T, block_out.reshape(query_rows.shape[0], -1))


def body(
    activations,
    attn_gain,
    w_qkv,
    w_gate,
    w_out,
    pair_bias,
    chain_ids,
    binder_flag,
    trans_gain,
    w_up,
    w_down,
):
    samples, own_rows, model_width = activations.shape
    head_count, query_count, key_count = pair_bias.shape
    pb_ratio = lax.axis_size("pb") // lax.axis_size("ka")
    normed = layer_norm(activations.astype(jnp.float32), attn_gain).astype(jnp.bfloat16)
    flat_normed = normed.reshape(-1, model_width)
    gate_pre = jnp.dot(flat_normed, w_gate, preferred_element_type=jnp.float32).reshape(
        samples, own_rows, model_width
    )
    queries = jnp.dot(flat_normed, w_qkv[:, :model_width], preferred_element_type=jnp.float32)
    queries = queries.astype(jnp.bfloat16).reshape(samples, own_rows, model_width)
    queries, block_normed = in_one_piece((queries, normed), "ka", 1, 0)
    input_parts = []
    for within in range(pb_ratio):
        source_index = lax.axis_index("ka") * pb_ratio + within
        input_parts.append(spread_2(block_normed, "pb", source_index))
    key_inputs = jnp.concatenate(input_parts, axis=1).reshape(-1, model_width)
    key_value = jnp.dot(key_inputs, w_qkv[:, model_width:], preferred_element_type=jnp.float32)
    key_block = (
        key_value[:, :model_width].astype(jnp.bfloat16).reshape(samples, key_count, model_width)
    )
    value_block = (
        key_value[:, model_width:].astype(jnp.bfloat16).reshape(samples, key_count, model_width)
    )
    query_start = lax.axis_index("pb") * query_count
    key_start = lax.axis_index("ka") * key_count
    row_chain = lax.dynamic_slice_in_dim(chain_ids, query_start, query_count, 0)
    row_binder = lax.dynamic_slice_in_dim(binder_flag, query_start, query_count, 0)
    col_chain = lax.dynamic_slice_in_dim(chain_ids, key_start, key_count, 0)
    col_binder = lax.dynamic_slice_in_dim(binder_flag, key_start, key_count, 0)
    allowed = (
        (row_binder[:, None] > 0)
        | (col_binder[None, :] > 0)
        | (row_chain[:, None] == col_chain[None, :])
    )

    def per_sample(operands):
        return block_stats(operands[0], operands[1], operands[2], pair_bias, allowed)

    block_tops, block_sums, block_outs = lax.map(per_sample, (queries, key_block, value_block))
    all_tops, all_sums, all_outs = (
        lax.all_to_all(block_tops[None], "ka", split_axis=2, concat_axis=0, tiled=True),
        lax.all_to_all(block_sums[None], "ka", split_axis=2, concat_axis=0, tiled=True),
        lax.all_to_all(block_outs[None], "ka", split_axis=2, concat_axis=0, tiled=True),
    )
    overall = jnp.max(all_tops, axis=0)
    factors = jnp.exp(all_tops - overall)
    row_sum = jnp.sum(factors * all_sums, axis=0)
    shaped = all_outs.reshape(all_outs.shape[:-1] + (head_count, -1))
    row_out = jnp.sum(factors[..., None] * shaped, axis=0).reshape(samples, own_rows, model_width)
    attention = (row_out.reshape(samples, own_rows, head_count, -1) / row_sum[..., None]).reshape(
        samples, own_rows, model_width
    )
    gated = (jax.nn.sigmoid(gate_pre) * attention).astype(jnp.bfloat16)
    mixed = activations.astype(jnp.float32) + jnp.dot(
        gated.reshape(-1, model_width), w_out, preferred_element_type=jnp.float32
    ).reshape(samples, own_rows, model_width)
    trans_normed = layer_norm(mixed, trans_gain).astype(jnp.bfloat16)
    both_parts = jnp.dot(
        trans_normed.reshape(-1, model_width), w_up, preferred_element_type=jnp.float32
    )
    hidden_width = w_down.shape[0]
    hidden = (jax.nn.silu(both_parts[:, :hidden_width]) * both_parts[:, hidden_width:]).astype(
        jnp.bfloat16
    )
    updated = mixed + jnp.dot(hidden, w_down, preferred_element_type=jnp.float32).reshape(
        samples, own_rows, model_width
    )
    return updated.astype(jnp.bfloat16)


def solution(mesh):
    placed = (
        P(None, ("pb", "ka"), None),
        P(),
        P(),
        P(),
        P(),
        P(None, "pb", "ka"),
        P(),
        P(),
        P(),
        P(),
        P(),
    )
    return jax.shard_map(
        body, mesh=mesh, in_specs=placed, out_specs=P(None, ("pb", "ka"), None), check_vma=False
    )
```

profile of v0, /device:TPU:1, one launch (start us, length us, event | category | flops | bytes accessed | tf_op | source)
XLA Modules:
  0.0 493.7 jit_solution(10470582669954090714)
XLA Ops:
  12.4 73.1 %all-gather.2.cloned.1.call-done = bf16[8,256,768]{2,1,0:T(8,128)(2,1)} async-done(((bf16[8,32,768]{2,1,0:T(8,128)(2,1)}), bf16[8,256,768]{2,1,0:T(8,128)(2,1)}) %all-gather.2.cloned.1.call-update) | async-done | bytes 3145744 | tf_op jit(solution)/shard_map/all_gather | solution.py:18
  85.6 4.2 broadcast_select_fusion.1
  92.8 148.8 %all-reduce.3.cloned.1.call-done = (bf16[4,256,768]{2,1,0:T(8,128)(2,1)}, bf16[4,256,768]{2,1,0:T(8,128)(2,1)}) async-done(((bf16[4,256,768]{2,1,0:T(8,128)(2,1)}, bf16[4,256,768]{2,1,0:T(8,128)(2,1)}), (bf16[4,256,768]{2,1,0:T(8,128)(2,1)}, bf16[4,256,768]{2,1,0:T(8,128)(2,1)})) %all-reduce.3.cloned.1.call-update) | async-done | bytes 3145744 | tf_op jit(solution)/shard_map/psum | solution.py:23
  244.6 5.4 %convolution_convert_fusion = bf16[2048,1536]{1,0:T(8,128)(2,1)S(1)} fusion(bf16[2048,768]{1,0:T(8,128)(2,1)S(1)} %bitcast.103, bf16[768,2304]{1,0:T(8,128)(2,1)S(1)} %copy-done.6), kind=kOutput, calls=%fused_computation.17 | convolution fusion | flops 4834983936 | bytes 11796480 | tf_op jit(solution)/shard_map/dot_general | solution.py:83
  253.1 158.6 %while.15 = (s32[]{:T(128)}, f32[4,256,16]{1,2,0:T(8,128)S(1)}, f32[4,256,16]{1,2,0:T(8,128)S(1)}, f32[4,256,768]{2,0,1:T(4,128)}, bf16[4,256,768]{2,1,0:T(8,128...) while((s32[]{:T(128)}, f32[4,256,16]{1,2,0:T(8,128)S(1)}, ...), condition=%wide.region_7.8_spmd.clone, body=%wide.region_4.7_spmd.clone.sunk | while | flops 426106880 | bytes 77336504 | solution.py:105
  257.6 4.9 select_reduce_fusion.2
  269.2 5.8 %fusion.71 = f32[16,48,256]{2,1,0:T(8,128)} fusion(bf16[512,16,48]{0,2,1:T(8,128)(2,1)S(1)} %bitcast.95, f32[16,256,512]{2,1,0:T(8,128)} %copy-done.1, f32[16,256]{1,0:T(8,128)S(1)} %get-tuple-element.240, pred[256,512]{1,0:T(8,128)(4,1)S(1)} %compare_or_fusion.2), kind=kOutput, calls=%fused_computation.6.clone.1 | convolution fusion | flops 207618048 | bytes 10108928 | tf_op jit(solution)/shard_map/while/body/eval_jaxpr/hqk,khd->qhd/dot_general | solution.py:45
  277.3 15.4 %dynamic_update_slice.19 = f32[4,256,768]{2,0,1:T(4,128)} dynamic-update-slice(f32[4,256,768]{2,0,1:T(4,128)} %get-tuple-element.260, f32[1,256,768]{2,0,1:T(1,128)S(1)} %copy.49, s32[]{:T(128)S(6)} %copy.59, s32[]{:T(128)} %constant.36.clone.1..sunk, s32[]{:T(128)} %constant.36.clone.1..sunk) | dynamic-update-slice | bytes 1572868 | tf_op jit(solution)/shard_map/while/body/jit(dynamic_update_index_in_dim)/dynamic_update_slice | solution.py:105
  297.2 4.9 select_reduce_fusion.2
  308.8 5.8 %fusion.71 = f32[16,48,256]{2,1,0:T(8,128)} fusion(bf16[512,16,48]{0,2,1:T(8,128)(2,1)S(1)} %bitcast.95, f32[16,256,512]{2,1,0:T(8,128)} %copy-done.1, f32[16,256]{1,0:T(8,128)S(1)} %get-tuple-element.240, pred[256,512]{1,0:T(8,128)(4,1)S(1)} %compare_or_fusion.2), kind=kOutput, calls=%fused_computation.6.clone.1 | convolution fusion | flops 207618048 | bytes 10108928 | tf_op jit(solution)/shard_map/while/body/eval_jaxpr/hqk,khd->qhd/dot_general | solution.py:45
  317.0 15.4 %dynamic_update_slice.19 = f32[4,256,768]{2,0,1:T(4,128)} dynamic-update-slice(f32[4,256,768]{2,0,1:T(4,128)} %get-tuple-element.260, f32[1,256,768]{2,0,1:T(1,128)S(1)} %copy.49, s32[]{:T(128)S(6)} %copy.59, s32[]{:T(128)} %constant.36.clone.1..sunk, s32[]{:T(128)} %constant.36.clone.1..sunk) | dynamic-update-slice | bytes 1572868 | tf_op jit(solution)/shard_map/while/body/jit(dynamic_update_index_in_dim)/dynamic_update_slice | solution.py:105
  336.9 4.9 select_reduce_fusion.2
  348.5 5.8 %fusion.71 = f32[16,48,256]{2,1,0:T(8,128)} fusion(bf16[512,16,48]{0,2,1:T(8,128)(2,1)S(1)} %bitcast.95, f32[16,256,512]{2,1,0:T(8,128)} %copy-done.1, f32[16,256]{1,0:T(8,128)S(1)} %get-tuple-element.240, pred[256,512]{1,0:T(8,128)(4,1)S(1)} %compare_or_fusion.2), kind=kOutput, calls=%fused_computation.6.clone.1 | convolution fusion | flops 207618048 | bytes 10108928 | tf_op jit(solution)/shard_map/while/body/eval_jaxpr/hqk,khd->qhd/dot_general | solution.py:45
  356.6 15.4 %dynamic_update_slice.19 = f32[4,256,768]{2,0,1:T(4,128)} dynamic-update-slice(f32[4,256,768]{2,0,1:T(4,128)} %get-tuple-element.260, f32[1,256,768]{2,0,1:T(1,128)S(1)} %copy.49, s32[]{:T(128)S(6)} %copy.59, s32[]{:T(128)} %constant.36.clone.1..sunk, s32[]{:T(128)} %constant.36.clone.1..sunk) | dynamic-update-slice | bytes 1572868 | tf_op jit(solution)/shard_map/while/body/jit(dynamic_update_index_in_dim)/dynamic_update_slice | solution.py:105
  376.6 4.9 select_reduce_fusion.2
  388.2 5.8 %fusion.71 = f32[16,48,256]{2,1,0:T(8,128)} fusion(bf16[512,16,48]{0,2,1:T(8,128)(2,1)S(1)} %bitcast.95, f32[16,256,512]{2,1,0:T(8,128)} %copy-done.1, f32[16,256]{1,0:T(8,128)S(1)} %get-tuple-element.240, pred[256,512]{1,0:T(8,128)(4,1)S(1)} %compare_or_fusion.2), kind=kOutput, calls=%fused_computation.6.clone.1 | convolution fusion | flops 207618048 | bytes 10108928 | tf_op jit(solution)/shard_map/while/body/eval_jaxpr/hqk,khd->qhd/dot_general | solution.py:45
  396.3 15.4 %dynamic_update_slice.19 = f32[4,256,768]{2,0,1:T(4,128)} dynamic-update-slice(f32[4,256,768]{2,0,1:T(4,128)} %get-tuple-element.260, f32[1,256,768]{2,0,1:T(1,128)S(1)} %copy.49, s32[]{:T(128)S(6)} %copy.59, s32[]{:T(128)} %constant.36.clone.1..sunk, s32[]{:T(128)} %constant.36.clone.1..sunk) | dynamic-update-slice | bytes 1572868 | tf_op jit(solution)/shard_map/while/body/jit(dynamic_update_index_in_dim)/dynamic_update_slice | solution.py:105
  413.1 4.0 all-to-all-start.2
  417.8 4.4 all-to-all-done.2
  422.2 7.7 %all_to_all.51 = f32[8,1,2048]{2,1,0:T(1,128)S(1)} all-to-all(f32[8,1,2048]{2,1,0:T(1,128)S(1)} %reshape.106), channel_id=1, replica_groups=mesh['pb'=16,'ka'=8] {'ka'}, dimensions={0} | all-to-all | bytes 131072 | tf_op jit(solution)/shard_map/all_to_all | solution.py:107
  429.9 4.5 all-to-all-start.1
  438.2 4.6 mul.80
  442.7 7.7 %mul.81 = f32[8,1,4,32,768]{4,3,0,2,1:T(8,128)} reshape(f32[8,4,32,16,48]{4,3,2,0,1:T(8,128)} %mul.80) | data formatting | bytes 6291456 | tf_op jit(solution)/shard_map/mul | solution.py:115
  452.0 23.7 %all-to-all-done.1 = f32[1,4,256,768]{3,1,0,2:T(4,128)} async-done(((f32[1,4,256,768]{3,1,0,2:T(4,128)}), f32[1,4,256,768]{3,1,0,2:T(4,128)}, u32[]{:S(2)}, u32[]{:S(2)}) %all-to-all-start.1) | async-done | bytes 3145760 | tf_op jit(solution)/shard_map/all_to_all | solution.py:109
  (109 shorter events, 87.3 us)
Async XLA Ops:
  6.5 479.0 %copy-start = (bf16[1536,768]{1,0:T(8,128)(2,1)S(1)}, bf16[1536,768]{1,0:T(8,128)(2,1)}, u32[]{:S(2)}) copy-start(bf16[1536,768]{1,0:T(8,128)(2,1)} %param.23) | copy-start | bytes 7077892
  6.5 79.0 %all-gather.2.cloned.1.call-start = ((), (), s32[]{:S(2)}) async-start(), calls=%async_computation.3 | async-start | bytes 3538944 | tf_op jit(solution)/shard_map/all_gather | solution.py:18
  12.4 229.3 %all-reduce.3.cloned.1.call-start = ((), (), s32[]{:S(2)}) async-start(), calls=%async_computation.4 | async-start | bytes 6291456 | tf_op jit(solution)/shard_map/psum | solution.py:23
  241.7 2.9 copy-start.6
  262.5 3.2 copy-start.1
  302.1 3.2 copy-start.1
  341.8 3.2 copy-start.1
  381.4 3.2 copy-start.1
  413.1 9.1 %all-to-all-start.2 = ((f32[8,1,2048]{2,1,0:T(1,128)}), f32[8,1,2048]{2,1,0:T(1,128)S(1)}, u32[]{:S(2)}, u32[]{:S(2)}) async-start(f32[8,1,2048]{2,1,0:T(1,128)} %reshape.108), calls=%async_computation.2 | async-start | bytes 131072 | tf_op jit(solution)/shard_map/all_to_all | solution.py:108
  429.9 45.9 %all-to-all-start.1 = ((f32[1,4,256,768]{3,1,0,2:T(4,128)}), f32[1,4,256,768]{3,1,0,2:T(4,128)}, u32[]{:S(2)}, u32[]{:S(2)}) async-start(f32[1,4,256,768]{3,1,0,2:T(4,128)} %bitcast.102), calls=%async_computation.1 | async-start | bytes 6291456 | tf_op jit(solution)/shard_map/all_to_all | solution.py:109
  475.7 2.8 copy-start.2
  478.6 0.9 copy-start.3
  478.6 0.9 copy-start.4
  479.5 2.8 copy-start.5
Sparse Core Ops, SparseCore 0:
  12.5 73.0 all-gather.1
  89.9 151.7 all-reduce.2
where the time goes:
time: 501 us; the launch traced here: 494 us
  waiting for transfers between devices  250 us (50%)
  local copies, waits for them, and re-layouts  132 us (26%)
  matrix products  56.1 us (11%)
  other arithmetic  25.7 us (5%)
  between operations  13.7 us (3%)
  starting transfers between devices  8.53 us (2%)
  blocking collectives  7.65 us (2%)
    psum x1, waiting for transfers between devices, spread_2(): return lax.psum(kept, axis)  149 us
    all_gather x1, waiting for transfers between devices, in_one_piece(): lax.all_gather(both, axis, axis=dim, tiled=True)  73.1 us
    dynamic_update_slice x12, local copies, waits for them, and re-layouts, body(): lax.map(per_sample, (queries, key_block, value_block))  71 us
    dynamic_slice x24, local copies, waits for them, and re-layouts, body(): lax.map(per_sample, (queries, key_block, value_block))  31.1 us
    all_to_all x1, waiting for transfers between devices, body(): lax.all_to_all(block_outs[None], 'ka', split_axis=2, concat_axis=0, tiled...  23.7 us
    dot_general x4, matrix products, block_stats(): jnp.einsum('hqk,khd->qhd', weights.astype(jnp.bfloat16), value_heads, pre...  23.3 us
    dot_general x4, matrix products, block_stats(): jnp.einsum('qhd,khd->hqk', query_heads, key_heads, preferred_element_type...  19.5 us
    mul x2, local copies, waits for them, and re-layouts, body(): factors[..., None] * shaped  12.3 us
  transfers between devices with their start and end apart: 4, of which 4 were waited for; matrix products, arithmetic and copies ran while one was open for 4% of the time, Pallas kernels for 0%

commit v1 on v0

v1 whole, which is shorter than its diff:
```python
import math

import jax
import jax.numpy as jnp
from jax import lax
from jax.experimental import pallas as pl
from jax.experimental.pallas import tpu as pltpu
from jax.sharding import PartitionSpec as P

EPS = 1e-5
LOG2E = 1.4426950408889634
MASKED = -1e9 * LOG2E
S, ROWS, D, H, HD = 4, 32, 768, 16, 48
NQ, NK, FF = 256, 512, 1536
WIDE = 896
QSCALE = LOG2E / math.sqrt(HD)
BF, F32 = jnp.bfloat16, jnp.float32
MESH = pl.DeviceIdType.MESH


def dot(a, b):
    return jnp.dot(a, b, preferred_element_type=F32)


def dot_t(a, b):
    return lax.dot_general(a, b, (((1,), (1,)), ((), ())), preferred_element_type=F32)


def norm(values, gain):
    centred = values - jnp.mean(values, axis=-1, keepdims=True)
    spread = jnp.mean(centred * centred, axis=-1, keepdims=True)
    return centred * lax.rsqrt(spread + EPS) * gain


def eye(n):
    return (
        lax.broadcasted_iota(jnp.int32, (n, n), 0) == lax.broadcasted_iota(jnp.int32, (n, n), 1)
    ).astype(F32).astype(BF)


def kernel(
    act, gain1, wqkv_h, wgate_h, wout_h, bias_h, chain, binder, gain2, wup_h, wdown_h,
    out,
    xq, xk, rl, wqkv, wgate, wout, wup, wdown, bias, bt, wqt, wvt, wkp, qtp, kp, vt,
    st, ot, lse, msg, rbuf, gate,
    wsem, p1s, p1r, zs, zr, crs, rls, rlr, ds, dr, rss, rsr,
):
    pb, ka = lax.axis_index("pb"), lax.axis_index("ka")
    z, core = pb // 4, pb % 2
    x, ylo = ka // 2, ka % 2
    yhi = (pb // 2) % 2
    r = (z - x + 4) % 4
    same = yhi == ylo
    root = jnp.logical_and(same, r == 0)
    cross0 = jnp.logical_and(jnp.logical_not(same), r == 0)
    cross1 = jnp.logical_and(jnp.logical_not(same), r % 2 == 1)
    not_root = jnp.logical_not(root)
    fwd_a = jnp.logical_and(not_root, r != 3)
    fwd_b = jnp.logical_and(not_root, r != 1)
    side = jnp.where(r == 1, 0, 2)
    xp, xm = (ka + 2) % 8, (ka + 6) % 8
    mate = x * 2 + (1 - ylo)
    zp, zm = (pb + 4) % 16, (pb + 12) % 16
    twin = (pb // 2) * 2 + (1 - core)
    opp = (z * 4 + (1 - yhi) * 2 + core, mate)
    relay_to = jnp.where(r == 1, xp, xm)

    def rcopy(src, dst, ssem, rsem, dev):
        return pltpu.make_async_remote_copy(
            src_ref=src, dst_ref=dst, send_sem=ssem, recv_sem=rsem,
            device_id=dev, device_id_type=MESH,
        )

    local = [
        pltpu.make_async_copy(a, b, wsem.at[i])
        for i, (a, b) in enumerate(
            ((wqkv_h, wqkv), (bias_h, bias), (wgate_h, wgate), (wout_h, wout), (wup_h, wup), (wdown_h, wdown))
        )
    ]
    for c in local:
        c.start()

    for s in range(S):
        xq[s, ka] = norm(act[s].astype(F32), gain1[...]).astype(BF)

    barrier = pltpu.get_barrier_semaphore()
    for i in range(1, 8):
        pl.semaphore_signal(barrier, inc=1, device_id=(pb, (ka + i) % 8), device_id_type=MESH)
    for dev in ((zp, ka), (zm, ka), (twin, ka), opp):
        pl.semaphore_signal(barrier, inc=1, device_id=dev, device_id_type=MESH)
    pl.semaphore_wait(barrier, 11)

    def slice_of(dx, dy):
        y = ylo if dy == 0 else 1 - ylo
        return ((x + dx) % 4) * 2 + y

    def p1(s, n, owner, dev, dx, dy):
        return rcopy(xq.at[s, owner], xq.at[s, owner], p1s.at[s, n], p1r.at[s, dx, dy], dev)

    def own_sends(s):
        return [
            p1(s, 0, ka, (pb, mate), 0, 1),
            p1(s, 1, ka, (pb, xp), 3, 0),
            p1(s, 2, ka, (pb, xm), 1, 0),
        ]

    def mate_sends(s):
        return [
            p1(s, 3, mate, (pb, xp), 3, 1),
            p1(s, 4, mate, (pb, xm), 1, 1),
        ]

    def far_send(s, up):
        if up:
            return p1(s, 5, slice_of(3, 0), (pb, xp), 2, 0)
        return p1(s, 6, slice_of(1, 1), (pb, xm), 2, 1)

    def p1_wait(s, dx, dy):
        o = slice_of(dx, dy)
        rcopy(xq.at[s, o], xq.at[s, o], p1s.at[s, 0], p1r.at[s, dx, dy], (pb, mate)).wait_recv()

    def own(s):
        for c in own_sends(s):
            c.start()

    def pass_on(s):
        p1_wait(s, 0, 1)
        for c in mate_sends(s):
            c.start()
        p1_wait(s, 3, 0)
        far_send(s, True).start()
        p1_wait(s, 1, 1)
        far_send(s, False).start()

    def gathered(s):
        for dx, dy in ((1, 0), (3, 1), (2, 0), (2, 1)):
            p1_wait(s, dx, dy)

    def piece(s, p):
        return xk.at[s, core, pl.ds(2 * p, 2)]

    def root_sends(s):
        cs = []
        for p in range(4):
            cs.append(rcopy(xq.at[s, pl.ds(2 * p, 2)], piece(s, p), zs.at[s, p], zr.at[s, p], (zp if p < 2 else zm, ka)))
        return cs

    def cross_sends(s):
        return [
            rcopy(xq.at[s, pl.ds(2 * p, 2)], piece(s, p), crs.at[s, p // 2], zr.at[s, p], opp) for p in (1, 3)
        ]

    def side_send(s):
        return rcopy(xq.at[s, pl.ds(2 * side, 2)], rl.at[s], crs.at[s, 0], rlr.at[s], opp)

    def relay_send(s):
        return rcopy(rl.at[s], piece(s, side), rls.at[s], zr.at[s, side], (pb, relay_to))

    def pass_send(s, p):
        return rcopy(piece(s, p), piece(s, p), zs.at[s, p], zr.at[s, p], (zp if p < 2 else zm, ka))

    def twin_send(s, src):
        return rcopy(src, xk.at[s, core], ds.at[s], dr.at[s], (twin, ka))

    def roots(s):
        @pl.when(root)
        def _():
            for c in root_sends(s):
                c.start()
            twin_send(s, xq.at[s]).start()
            xk[s, core] = xq[s]

        @pl.when(cross0)
        def _():
            for c in cross_sends(s):
                c.start()

        @pl.when(cross1)
        def _():
            side_send(s).start()

    def relay(s):
        @pl.when(cross1)
        def _():
            rcopy(rl.at[s], rl.at[s], crs.at[s, 0], rlr.at[s], opp).wait_recv()
            relay_send(s).start()

    def spread(s):
        for p in (0, 2, 1, 3):
            @pl.when(not_root)
            def _():
                pass_send(s, p).wait_recv()

            @pl.when(fwd_a if p < 2 else fwd_b)
            def _():
                pass_send(s, p).start()

        @pl.when(not_root)
        def _():
            twin_send(s, xk.at[s, core]).start()

    def prep_weights():
        local[0].wait()
        e = eye(256)
        for i in range(3):
            wqt[256 * i:256 * i + 256, :] = dot_t(e, wqkv[:, 256 * i:256 * i + 256]).astype(BF)
            wvt[256 * i:256 * i + 256, :] = dot_t(e, wqkv[:, 2 * D + 256 * i:2 * D + 256 * i + 256]).astype(BF)
        row = lax.broadcasted_iota(jnp.int32, (256, 256), 0)
        col = lax.broadcasted_iota(jnp.int32, (256, 256), 1)
        source = (col // 64) * HD + col % 64
        for t in range(4):
            start, off = (384 * (t // 2), 0) if t % 2 == 0 else (384 * (t // 2) + 128, 64)
            pick = jnp.logical_and(row == source + off, col % 64 < HD).astype(F32).astype(BF)
            wkp[:, 256 * t:256 * t + 256] = dot(wqkv[:, D + start:D + start + 256], pick).astype(BF)
        qtp[...] = jnp.zeros_like(qtp)
        tail = lax.broadcasted_iota(jnp.int32, (16, 16, NK), 1)
        ot[D + 48:, :] = jnp.zeros((WIDE - D - 48, NQ), BF)
        vt[:, HD:64, :] = (tail == 0).astype(F32).astype(BF)

    def prep_bias():
        local[1].wait()
        qc, qb = chain[pl.ds(pb * 2, 2), :], binder[pl.ds(pb * 2, 2), :]
        kc, kb = chain[pl.ds(ka * 4, 4), :], binder[pl.ds(ka * 4, 4), :]

        def features(c, b, n, at):
            c = jnp.concatenate([c[i:i + 1] for i in range(n // 128)], axis=1)
            b = jnp.concatenate([b[i:i + 1] for i in range(n // 128)], axis=1)
            kind = lax.broadcasted_iota(jnp.int32, (16, n), 0)
            f = jnp.where(kind == c, 1.0, 0.0)
            f = jnp.where(kind == 6 + at, jnp.where(b > 0, 1.0, 0.0), f)
            return jnp.where(kind == 7 - at, 1.0, f).astype(BF)

        allow = lax.dot_general(
            features(kc, kb, NK, 1), features(qc, qb, NQ, 0), (((0,), (0,)), ((), ())), preferred_element_type=F32
        )
        st[0] = allow

        def head(h, carry):
            e = eye(256)
            for t in range(2):
                b = dot_t(e, bias[h, :, 256 * t:256 * t + 256]) * LOG2E
                bt[h, 256 * t:256 * t + 256, :] = jnp.where(st[0, 256 * t:256 * t + 256, :] > 0.5, b, MASKED)
            return carry

        lax.fori_loop(0, H, head, 0)

    def prep_gate():
        local[2].wait()
        n = xq[:, ka].reshape(S * ROWS, D)
        gate[...] = 1.0 / (1.0 + jnp.exp(-dot(n, wgate[...])))

    def attend(s):
        qs = xq[s].reshape(NQ, D)
        q = (dot_t(wqt[...], qs) * QSCALE).astype(BF)
        for h in range(H):
            off = 64 * (h % 2)
            qtp[h, off:off + HD, :] = q[HD * h:HD * h + HD]
        ks = xk[s].reshape(NK, D)
        for n in range(4):
            k = dot(ks, wkp[:, 256 * n:256 * n + 256]).astype(BF)
            kp[2 * n] = k[:, :128]
            kp[2 * n + 1] = k[:, 128:]
        for t in range(2):
            v = dot_t(wvt[...], ks[256 * t:256 * t + 256]).astype(BF)
            for h in range(H):
                vt[h, 0:HD, 256 * t:256 * t + 256] = v[HD * h:HD * h + HD]

        def pair(hp, carry):
            tops = []
            for j in range(2):
                h = 2 * hp + j
                top = None
                for c in range(4):
                    v = dot(kp[hp, 128 * c:128 * c + 128, :], qtp[h]) + bt[h, 128 * c:128 * c + 128, :]
                    st[j, 128 * c:128 * c + 128, :] = v
                    m = jnp.max(v.reshape(16, 8, NQ), axis=0)
                    top = m if top is None else jnp.maximum(top, m)
                tops.append(jnp.max(top, axis=0, keepdims=True))
            for j in range(2):
                h = 2 * hp + j
                w = jnp.exp2(st[j] - tops[j]).astype(BF)
                o = dot(vt[h], w)
                total = o[HD:HD + 1]
                ot[pl.ds(pl.multiple_of(HD * h, 16), HD), :] = (o[:HD] * (1.0 / total)).astype(BF)
                lse[pl.ds(h, 1), :] = tops[j] + jnp.log2(total)
            return carry

        lax.fori_loop(0, H // 2, pair, 0)
        rest = lse[...]
        for i in range(3):
            part = rest.astype(BF)
            ot[D + 16 * i:D + 16 * i + 16, :] = part
            rest = rest - part.astype(F32)
        e = eye(256)
        for t in range(4):
            lo, n = 256 * t, min(256, WIDE - 256 * t)
            msg[s, :, :, lo:lo + n] = dot_t(e, ot[lo:lo + n, :]).astype(BF).reshape(8, ROWS, n)
        rbuf[s, ka] = msg[s, ka]

    def rs_send(s, i):
        to = (ka + i) % 8
        return rcopy(msg.at[s, to], rbuf.at[s, ka], rss.at[s, i - 1], rsr.at[s, 8 - i], (pb, to))

    def rs_wait(s, i):
        frm = (ka + i) % 8
        rcopy(msg.at[s, frm], rbuf.at[s, frm], rss.at[s, 0], rsr.at[s, i], (pb, frm)).wait_recv()

    def finish():
        lane = lax.broadcasted_iota(jnp.int32, (128, 128), 1)
        row = lax.broadcasted_iota(jnp.int32, (128, 128), 0)
        gather = jnp.logical_and(row % 16 == lane % 16, row < 48).astype(F32).astype(BF)
        erow = lax.broadcasted_iota(jnp.int32, (128, D), 0)
        ecol = lax.broadcasted_iota(jnp.int32, (128, D), 1)
        expand = jnp.logical_and(ecol // HD == erow % 16, erow < 32).astype(F32).astype(BF)
        sums = [dot(rbuf[:, b, :, D:].reshape(S * ROWS, 128), gather) for b in range(8)]
        top = sums[0]
        for b in range(1, 8):
            top = jnp.maximum(top, sums[b])
        w = [jnp.exp2(v - top) for v in sums]
        total = w[0]
        for b in range(1, 8):
            total = total + w[b]
        inv = 1.0 / total
        acc = jnp.zeros((S * ROWS, D), F32)
        for b in range(8):
            v = w[b] * inv
            hi = v.astype(BF)
            low = (v - hi.astype(F32)).astype(BF)
            both = jnp.where(lane < 16, hi.astype(F32), jnp.where(lane < 32, low.astype(F32), 0.0)).astype(BF)
            acc = acc + dot(both, expand) * rbuf[:, b, :, :D].reshape(S * ROWS, D).astype(F32)
        gated = (gate[...] * acc).astype(BF)
        local[3].wait()
        mixed = act[...].reshape(S * ROWS, D).astype(F32) + dot(gated, wout[...])
        normed = norm(mixed, gain2[...]).astype(BF)
        local[4].wait()
        left = dot(normed, wup[:, :FF])
        right = dot(normed, wup[:, FF:])
        hidden = (left / (1.0 + jnp.exp(-left)) * right).astype(BF)
        local[5].wait()
        out[...] = (mixed + dot(hidden, wdown[...])).astype(BF).reshape(S, ROWS, D)

    own(0)
    own(1)
    prep_weights()
    pass_on(0)
    own(2)
    pass_on(1)
    own(3)
    gathered(0)
    roots(0)
    prep_bias()
    pass_on(2)
    gathered(1)
    roots(1)
    relay(0)
    pass_on(3)
    gathered(2)
    roots(2)
    relay(1)
    prep_gate()
    gathered(3)
    roots(3)
    relay(2)
    relay(3)
    spread(0)

    def step(s, carry):
        @pl.when(s < S - 1)
        def _():
            spread(s + 1)

        twin_recv(s)
        attend(s)
        for i in (4, 3, 5, 2, 6, 1, 7):
            rs_send(s, i).start()
        return carry

    def twin_recv(s):
        rcopy(xk.at[s, 1 - core], xk.at[s, 1 - core], ds.at[s], dr.at[s], (twin, ka)).wait_recv()

    lax.fori_loop(0, S, step, 0)

    for s in range(S):
        for i in range(1, 8):
            rs_wait(s, i)
    finish()

    for s in range(S):
        for c in own_sends(s) + mate_sends(s) + [far_send(s, True), far_send(s, False)]:
            c.wait_send()
        for i in range(1, 8):
            rs_send(s, i).wait_send()
        twin_send(s, xq.at[s]).wait_send()
        for p in range(4):
            @pl.when(jnp.logical_or(root, fwd_a if p < 2 else fwd_b))
            def _():
                pass_send(s, p).wait_send()

        @pl.when(cross0)
        def _():
            for c in cross_sends(s):
                c.wait_send()

        @pl.when(cross1)
        def _():
            side_send(s).wait_send()
            relay_send(s).wait_send()


def body(act, gain1, wqkv, wgate, wout, bias, chain, binder, gain2, wup, wdown):
    vmem = pl.BlockSpec(memory_space=pltpu.VMEM)
    hbm = pl.BlockSpec(memory_space=pl.ANY)
    dma, v = pltpu.SemaphoreType.DMA, pltpu.VMEM
    return pl.pallas_call(
        kernel,
        out_shape=jax.ShapeDtypeStruct((S, ROWS, D), BF),
        in_specs=[vmem, vmem, hbm, hbm, hbm, hbm, vmem, vmem, vmem, hbm, hbm],
        out_specs=vmem,
        scratch_shapes=[
            v((S, 8, ROWS, D), BF), v((S, 2, 8, ROWS, D), BF), v((S, 2, ROWS, D), BF),
            v((D, 3 * D), BF), v((D, D), BF), v((D, D), BF), v((D, 2 * FF), BF), v((FF, D), BF),
            v((H, NQ, NK), BF), v((H, NK, NQ), F32),
            v((D, D), BF), v((D, D), BF), v((D, 1024), BF),
            v((H, 128, NQ), BF), v((H // 2, NK, 128), BF), v((H, 64, NK), BF),
            v((2, NK, NQ), F32), v((WIDE, NQ), BF), v((H, NQ), F32),
            v((S, 8, ROWS, WIDE), BF), v((S, 8, ROWS, WIDE), BF), v((S * ROWS, D), F32),
            dma((6,)), dma((S, 7)), dma((S, 4, 2)), dma((S, 4)), dma((S, 4)), dma((S, 2)),
            dma((S,)), dma((S,)), dma((S,)), dma((S,)), dma((S, 7)), dma((S, 8)),
        ],
        compiler_params=pltpu.CompilerParams(
            collective_id=0, has_side_effects=True, vmem_limit_bytes=66_000_000
        ),
        name="block",
    )(
        act, gain1.reshape(1, D), wqkv, wgate, wout, bias, chain.reshape(32, 128), binder.reshape(32, 128),
        gain2.reshape(1, D), wup, wdown,
    )


def solution(mesh):
    placed = (
        P(None, ("pb", "ka"), None), P(), P(), P(), P(), P(None, "pb", "ka"), P(), P(), P(), P(), P(),
    )
    return jax.shard_map(
        body, mesh=mesh, in_specs=placed, out_specs=P(None, ("pb", "ka"), None), check_vma=False
    )
```

time: 501 us -> 206 us (0.41)
  the two profiles are of different devices: /device:TPU:1 before, /device:TPU:120 now
where the time goes in v1:
time: 206 us
  Pallas kernels  202 us (98%)
  local copies, waits for them, and re-layouts  4.15 us (2%)
    pallas_call x1, Pallas kernels, body(): pl.pallas_call(kernel, out_shape=jax.ShapeDtypeStruct((S, ROWS, D), BF),...  202 us

profile of v1, /device:TPU:120, one launch (start us, length us, event | category | flops | bytes accessed | tf_op | source)
XLA Modules:
  0.0 205.9 jit_solution(10274021923006015044)
XLA Ops:
  0.0 1.3 reshape.12.gain1
  1.3 1.3 reshape.15.gain2
  2.5 201.8 %block.1 = bf16[4,32,768]{2,1,0:T(8,128)(2,1)} custom-call(bf16[4,32,768]{2,1,0:T(8,128)(2,1)} %act.1, f32[1,768]{1,0:T(1,128)} %reshape.12.gain1, bf16[768,2304]{1,0:T(8,128)(2,1)} %wqkv_h.1, bf16[768,768]{1,0:T(8,128)(2,1)} %wgate_h.1, bf16[768,768]{1,0:T(8,128)(2,1)} %wout_h.1, bf16[16,256,512]{2,1,0:T(8,128)(2,1)} %bias_h.1, s32[32,128]{1,0:T(8,128)} %bitcast.2, ...), custom_call_target="tpu_custom_call" | custom-call | tf_op jit(solution)/shard_map/block/pallas_call | solution.py:414
  204.3 1.6 copy.13

commit v2 on v1

--- a/solution.py
+++ b/solution.py
@@ -57,7 +57,7 @@
     not_root = jnp.logical_not(root)
     fwd_a = jnp.logical_and(not_root, r != 3)
     fwd_b = jnp.logical_and(not_root, r != 1)
-    side = jnp.where(r == 1, 0, 2)
+    side = jnp.where(r == 1, 1, 3)
     xp, xm = (ka + 2) % 8, (ka + 6) % 8
     mate = x * 2 + (1 - ylo)
     zp, zm = (pb + 4) % 16, (pb + 12) % 16
@@ -147,7 +147,7 @@
 
     def cross_sends(s):
         return [
-            rcopy(xq.at[s, pl.ds(2 * p, 2)], piece(s, p), crs.at[s, p // 2], zr.at[s, p], opp) for p in (1, 3)
+            rcopy(xq.at[s, pl.ds(2 * p, 2)], piece(s, p), crs.at[s, p // 2], zr.at[s, p], opp) for p in (0, 2)
         ]
 
     def side_send(s):
@@ -185,18 +185,36 @@
             rcopy(rl.at[s], rl.at[s], crs.at[s, 0], rlr.at[s], opp).wait_recv()
             relay_send(s).start()
 
-    def spread(s):
-        for p in (0, 2, 1, 3):
-            @pl.when(not_root)
+    def hop(t):
+        late = jnp.where(same, 0, 3)
+        up = t - 2 * r - late
+        down = t - 2 * ((4 - r) % 4) - late
+
+        @pl.when(jnp.logical_and(not_root, jnp.logical_and(up >= 0, up < 2 * S)))
+        def _():
+            s, p = lax.div(up, 2), lax.rem(up, 2)
+            c = rcopy(piece(s, p), piece(s, p), zs.at[s, p], zr.at[s, p], (zp, ka))
+            c.wait_recv()
+
+            @pl.when(fwd_a)
             def _():
-                pass_send(s, p).wait_recv()
-
-            @pl.when(fwd_a if p < 2 else fwd_b)
+                c.start()
+
+        @pl.when(jnp.logical_and(not_root, jnp.logical_and(down >= 0, down < 2 * S)))
+        def _():
+            s, p = lax.div(down, 2), 2 + lax.rem(down, 2)
+            c = rcopy(piece(s, p), piece(s, p), zs.at[s, p], zr.at[s, p], (zm, ka))
+            c.wait_recv()
+
+            @pl.when(fwd_b)
             def _():
-                pass_send(s, p).start()
-
-        @pl.when(not_root)
-        def _():
+                c.start()
+
+        last = jnp.minimum(up, down)
+
+        @pl.when(jnp.logical_and(not_root, jnp.logical_and(jnp.logical_and(last >= 0, last < 2 * S), lax.rem(last, 2) == 1)))
+        def _():
+            s = lax.div(last, 2)
             twin_send(s, xk.at[s, core]).start()
 
     def prep_weights():
@@ -266,6 +284,10 @@
                 vt[h, 0:HD, 256 * t:256 * t + 256] = v[HD * h:HD * h + HD]
 
         def pair(hp, carry):
+            @pl.when(jnp.logical_and(s < S - 1, hp % 4 == 2))
+            def _():
+                hop(11 + 2 * s + hp // 4)
+
             tops = []
             for j in range(2):
                 h = 2 * hp + j
@@ -353,22 +375,25 @@
     gathered(1)
     roots(1)
     relay(0)
+    for t in range(4):
+        hop(t)
     pass_on(3)
     gathered(2)
     roots(2)
     relay(1)
+    for t in range(4, 6):
+        hop(t)
     prep_gate()
     gathered(3)
     roots(3)
     relay(2)
+    for t in range(6, 8):
+        hop(t)
     relay(3)
-    spread(0)
+    for t in range(8, 11):
+        hop(t)
 
     def step(s, carry):
-        @pl.when(s < S - 1)
-        def _():
-            spread(s + 1)
-
         twin_recv(s)
         attend(s)
         for i in (4, 3, 5, 2, 6, 1, 7):

time: 206 us -> 90 us (0.44)
  the two profiles are of different devices: /device:TPU:120 before, /device:TPU:1 now
where the time goes in v2:
time: 90 us; the launch traced here: 89.8 us
  Pallas kernels  85.7 us (95%)
  local copies, waits for them, and re-layouts  4.15 us (5%)
    pallas_call x1, Pallas kernels, body(): pl.pallas_call(kernel, out_shape=jax.ShapeDtypeStruct((S, ROWS, D), BF),...  85.7 us

profile of v2, /device:TPU:1, one launch (start us, length us, event | category | flops | bytes accessed | tf_op | source)
XLA Modules:
  0.0 89.8 jit_solution(17747702041526292796)
XLA Ops:
  0.0 1.3 %reshape.12.gain1 = f32[1,768]{1,0:T(1,128)} reshape(f32[768]{0:T(1024)} %param.12) | data formatting | bytes 6144 | tf_op jit(solution)/shard_map/reshape | solution.py:460
  1.3 1.3 %reshape.15.gain2 = f32[1,768]{1,0:T(1,128)} reshape(f32[768]{0:T(1024)} %param.19) | data formatting | bytes 6144 | tf_op jit(solution)/shard_map/reshape | solution.py:461
  2.5 85.7 %block.1 = bf16[4,32,768]{2,1,0:T(8,128)(2,1)} custom-call(bf16[4,32,768]{2,1,0:T(8,128)(2,1)} %act.1, f32[1,768]{1,0:T(1,128)} %reshape.12.gain1, bf16[768,2304]{1,0:T(8,128)(2,1)} %wqkv_h.1, bf16[768,768]{1,0:T(8,128)(2,1)} %wgate_h.1, bf16[768,768]{1,0:T(8,128)(2,1)} %wout_h.1, bf16[16,256,512]{2,1,0:T(8,128)(2,1)} %bias_h.1, s32[32,128]{1,0:T(8,128)} %bitcast.2, ...), custom_call_target="tpu_custom_call" | custom-call | tf_op jit(solution)/shard_map/block/pallas_call | solution.py:439
  88.2 1.6 %copy.13 = bf16[4,32,768]{2,1,0:T(8,128)(2,1)} copy(bf16[4,32,768]{2,1,0:T(8,128)(2,1)} %block.1) | data formatting | bytes 393216

commit v3 on v1

v3 whole, which is shorter than its diff:
```python
import math

import jax
import jax.numpy as jnp
from jax import lax
from jax.experimental import pallas as pl
from jax.experimental.pallas import tpu as pltpu
from jax.sharding import PartitionSpec as P

EPS = 1e-5
LOG2E = 1.4426950408889634
MASKED = -1e9 * LOG2E
S, ROWS, D, H, HD = 4, 32, 768, 16, 48
NQ, NK, FF = 256, 512, 1536
QSCALE = LOG2E / math.sqrt(HD)
BF, F32 = jnp.bfloat16, jnp.float32
MESH = pl.DeviceIdType.MESH


def dot(a, b):
    return jnp.dot(a, b, preferred_element_type=F32)


def dot_t(a, b):
    return lax.dot_general(a, b, (((1,), (1,)), ((), ())), preferred_element_type=F32)


def norm(values, gain):
    centred = values - jnp.mean(values, axis=-1, keepdims=True)
    spread = jnp.mean(centred * centred, axis=-1, keepdims=True)
    return centred * lax.rsqrt(spread + EPS) * gain


def eye(n):
    return (
        lax.broadcasted_iota(jnp.int32, (n, n), 0) == lax.broadcasted_iota(jnp.int32, (n, n), 1)
    ).astype(F32).astype(BF)


UP = ((0, 0), (1, 0), (1, 1), (2, 0))
DOWN = ((0, 1), (3, 0), (3, 1), (2, 1))
CLASSES = [(e, r) for e in (1, 0) for r in range(4)]


def slot(dx, dy):
    return UP.index((dx, dy)) if (dx, dy) in UP else 4 + DOWN.index((dx, dy))


def rank(op):
    s, kind = op[1], op[0]
    if kind in ("own", "mate", "far", "relay"):
        return s + ("own", "mate", "far", "relay").index(kind)
    return 10 * s + (op[3] if kind == "z" else op[2])


def traffic(occupied=23, latency=44):
    have = {c: {} for c in CLASSES}
    pend, free, log = {}, {}, {c: [] for c in CLASSES}
    for c in CLASSES:
        e, r = c
        ops = {l: [] for l in ("x+", "x-", "y", "o", "z+", "z-")}
        for s in range(S):
            have[c]["q", s, 0, 0] = 0
            ops["y"].append((("own", s), ("q", s, 0, 0)))
            for d in ("x+", "x-"):
                ops[d].append((("own", s), ("q", s, 0, 0)))
                ops[d].append((("mate", s), ("q", s, 0, 1)))
            ops["x+"].append((("far", s), ("q", s, 3, 0)))
            ops["x-"].append((("far", s), ("q", s, 1, 1)))
            for d, owners, end in (("z+", UP, 3), ("z-", DOWN, 1)):
                for g in range(4):
                    if r != end:
                        ops[d].append((("z", s, d, g), ("q" if c == (1, 0) else "k", s) + owners[g]))
            if c == (0, 0):
                ops["o"] += [(("cross", s, dx, dy), ("q", s, dx, dy)) for dx in (0, 2) for dy in (0, 1)]
            if e == 0 and r in (1, 3):
                for dy in (0, 1):
                    ops["o"].append((("side", s, dy), ("q", s, 0, dy)))
                    ops["x+" if r == 1 else "x-"].append((("relay", s, dy), ("rl", s, dy)))
        pend[c] = ops
        free.update({(c, l): 0 for l in ops})
    for now in range(2000):
        for c in CLASSES:
            e, r = c
            for l, ops in pend[c].items():
                ready = [o for o in ops if have[c].get(o[1], now + 1) <= now]
                if free[c, l] > now or not ready:
                    continue
                o = min(ready, key=lambda o: rank(o[0]))
                ops.remove(o)
                free[c, l] = now + occupied
                op, s = o[0], o[0][1]
                log[c].append((now, op, o[1], l))
                step = {"x+": -1, "x-": 1, "z+": 1, "z-": -1}.get(l, 0)
                to = (1 - e if l == "y" else e, (r + step) % 4)
                if op[0] == "z":
                    item = ("k",) + o[1][1:]
                elif op[0] == "cross":
                    item = ("k",) + op[1:]
                elif op[0] == "side":
                    item = ("rl",) + op[1:]
                elif op[0] == "relay":
                    item = ("k", s, 3 if r == 1 else 1, op[2])
                elif l == "y":
                    item = ("q", s, 0, 1)
                elif op[0] == "far":
                    item = ("q", s, 2, 0 if l == "x+" else 1)
                else:
                    item = ("q", s, 3 if l == "x+" else 1, 0 if op[0] == "own" else 1)
                assert item not in have[to]
                have[to][item] = now + occupied + latency
    plans = {}
    for c in CLASSES:
        assert not any(pend[c].values())
        events = [(t, ("send",) + tuple(rest)) for t, *rest in log[c]]
        for s in range(S):
            for kind in ("q", "k"):
                items = [(kind, s, dx, dy) for dx in range(4) for dy in range(2)]
                if kind == "k" and c == (1, 0):
                    continue
                at = max(have[c][i] for i in items)
                events.append((at, ("all", kind, s, items)))
                if kind == "k" or c == (1, 0):
                    events.append((at, ("twin", s)))
        events.sort(key=lambda v: v[0])
        waited = {("q", s, 0, 0) for s in range(S)}
        plan = []
        for at, ev in events:
            needs = ev[3] if ev[0] == "all" else [ev[2]] if ev[0] == "send" else []
            for item in needs:
                if item not in waited:
                    waited.add(item)
                    plan.append((at, ("wait", item)))
            if ev[0] != "all":
                plan.append((at, ev))
        plans[c] = plan
    return plans


def kernel(
    act, gain1, wqkv_h, wgate_h, wout_h, bias_h, chain, binder, gain2, wup_h, wdown_h,
    out,
    xq, xk, rl, wqkv, wgate, wout, wup, wdown, bias, bt, wqt, wvt, wkp, qtp, kp, vt,
    st, ot, lse, msg, rbuf, smsg, srbuf, ost, gate,
    wsem, p1s, p1r, zs, zr, crs, rls, rlr, ds, dr, rss, rsr, sss, ssr,
):
    pb, ka = lax.axis_index("pb"), lax.axis_index("ka")
    z, core = pb // 4, pb % 2
    x, ylo = ka // 2, ka % 2
    yhi = (pb // 2) % 2
    r = (z - x + 4) % 4
    same = yhi == ylo
    odd = jnp.where(same, 0, 1)
    xp, xm = (ka + 2) % 8, (ka + 6) % 8
    mate = x * 2 + (1 - ylo)
    zp, zm = (pb + 4) % 16, (pb + 12) % 16
    twin = (pb // 2) * 2 + (1 - core)
    opp = (z * 4 + (1 - yhi) * 2 + core, mate)

    def rcopy(src, dst, ssem, rsem, dev):
        return pltpu.make_async_remote_copy(
            src_ref=src, dst_ref=dst, send_sem=ssem, recv_sem=rsem,
            device_id=dev, device_id_type=MESH,
        )

    local = [
        pltpu.make_async_copy(a, b, wsem.at[i])
        for i, (a, b) in enumerate(
            ((wqkv_h, wqkv), (bias_h, bias), (wgate_h, wgate), (wout_h, wout), (wup_h, wup), (wdown_h, wdown))
        )
    ]
    for c in local:
        c.start()

    barrier = pltpu.get_barrier_semaphore()
    for i in range(1, 8):
        pl.semaphore_signal(barrier, inc=1, device_id=(pb, (ka + i) % 8), device_id_type=MESH)
    for dev in ((zp, ka), (zm, ka), (twin, ka), opp):
        pl.semaphore_signal(barrier, inc=1, device_id=dev, device_id_type=MESH)

    for s in range(S):
        xq[s, ka] = norm(act[s].astype(F32), gain1[...].reshape(1, D)).astype(BF)

    pl.semaphore_wait(barrier, 11)

    def q_at(dx, dy):
        return ((x + dx) % 4) * 2 + (ylo + dy) % 2

    def k_at(dx, dy):
        return ((x + dx) % 4) * 2 + (ylo + dy + odd) % 2

    def sent(c, op, item, link):
        kind, s = op[0], op[1]
        if kind in ("own", "mate", "far"):
            ref = xq.at[s, q_at(*item[2:])]
            up = link == "x+"
            if link == "y":
                n, sem, to = 0, (0, 1), mate
            else:
                to = xp if up else xm
                n = {"own": 1, "mate": 3, "far": 5}[kind] + (0 if up else 1)
                if kind == "far":
                    sem = (2, 0 if up else 1)
                else:
                    sem = (3 if up else 1, 0 if kind == "own" else 1)
            return rcopy(ref, ref, p1s.at[s, n], p1r.at[s, sem[0], sem[1]], (pb, to))
        if kind == "z":
            owner = item[2:]
            at = k_at(*owner)
            n = slot(*owner)
            src = xq if item[0] == "q" else xk.at[:, core]
            return rcopy(src.at[s, at], xk.at[s, core, at], zs.at[s, n], zr.at[s, n], (zp if link == "z+" else zm, ka))
        if kind == "cross":
            at = q_at(*item[2:])
            return rcopy(xq.at[s, at], xk.at[s, core, at], crs.at[s, op[2] + op[3]], zr.at[s, slot(*item[2:])], opp)
        dy = op[2]
        if kind == "side":
            return rcopy(xq.at[s, q_at(0, dy)], rl.at[s, dy], crs.at[s, dy], rlr.at[s, dy], opp)
        n = slot(3 if c[1] == 1 else 1, dy)
        return rcopy(rl.at[s, dy], xk.at[s, core, k_at(0, dy)], rls.at[s, dy], zr.at[s, n], (pb, xp if c[1] == 1 else xm))

    def arrived(item):
        s = item[1]
        if item[0] == "q":
            ref, ssem, rsem = xq.at[s, q_at(*item[2:])], p1s.at[s, 0], p1r.at[s, item[2], item[3]]
        elif item[0] == "k":
            n = slot(*item[2:])
            ref, ssem, rsem = xk.at[s, core, k_at(*item[2:])], zs.at[s, n], zr.at[s, n]
        else:
            ref, ssem, rsem = rl.at[s, item[2]], rls.at[s, item[2]], rlr.at[s, item[2]]
        rcopy(ref, ref, ssem, rsem, opp).wait_recv()

    def twin_send(s, src):
        return rcopy(src, xk.at[s, core], ds.at[s], dr.at[s], (twin, ka))

    plans = traffic()

    def each_class(body):
        for c in CLASSES:
            @pl.when(jnp.logical_and(odd == 1 - c[0], r == c[1]))
            def _():
                body(c)

    done = [0]

    def until(us):
        low, high = done[0], int(us * 20)
        done[0] = high
        for c in CLASSES:
            events = [ev for at, ev in plans[c] if low <= at < high]
            if not events:
                continue

            @pl.when(jnp.logical_and(odd == 1 - c[0], r == c[1]))
            def _():
                for ev in events:
                    if ev[0] == "wait":
                        arrived(ev[1])
                    elif ev[0] == "send":
                        sent(c, *ev[1:]).start()
                    elif c == (1, 0):
                        twin_send(ev[1], xq.at[ev[1]]).start()
                        xk[ev[1], core] = xq[ev[1]]
                    else:
                        twin_send(ev[1], xk.at[ev[1], core]).start()

    def turn_query_weights():
        local[0].wait()
        e = eye(256)
        for i in range(3):
            wqt[256 * i:256 * i + 256, :] = dot_t(e, wqkv[:, 256 * i:256 * i + 256]).astype(BF)
        qtp[...] = jnp.zeros_like(qtp)

    def turn_value_weights():
        e = eye(256)
        for i in range(3):
            wvt[256 * i:256 * i + 256, :] = dot_t(e, wqkv[:, 2 * D + 256 * i:2 * D + 256 * i + 256]).astype(BF)
        ost[...] = jnp.zeros_like(ost)
        tail = lax.broadcasted_iota(jnp.int32, (16, 16, NK), 1)
        vt[:, HD:64, :] = (tail == 0).astype(F32).astype(BF)

    def pad_key_weights():
        row = lax.broadcasted_iota(jnp.int32, (256, 256), 0)
        col = lax.broadcasted_iota(jnp.int32, (256, 256), 1)
        source = (col // 64) * HD + col % 64
        for t in range(4):
            start, off = (384 * (t // 2), 0) if t % 2 == 0 else (384 * (t // 2) + 128, 64)
            pick = jnp.logical_and(row == source + off, col % 64 < HD).astype(F32).astype(BF)
            wkp[:, 256 * t:256 * t + 256] = dot(wqkv[:, D + start:D + start + 256], pick).astype(BF)

    def prep_bias():
        local[1].wait()
        qc, qb = chain[pl.ds(pb * 2, 2), :], binder[pl.ds(pb * 2, 2), :]
        kc, kb = chain[pl.ds(ka * 4, 4), :], binder[pl.ds(ka * 4, 4), :]

        def features(c, b, n, at):
            c = jnp.concatenate([c[i:i + 1] for i in range(n // 128)], axis=1)
            b = jnp.concatenate([b[i:i + 1] for i in range(n // 128)], axis=1)
            kind = lax.broadcasted_iota(jnp.int32, (16, n), 0)
            f = jnp.where(kind == c, 1.0, 0.0)
            f = jnp.where(kind == 6 + at, jnp.where(b > 0, 1.0, 0.0), f)
            return jnp.where(kind == 7 - at, 1.0, f).astype(BF)

        allow = lax.dot_general(
            features(kc, kb, NK, 1), features(qc, qb, NQ, 0), (((0,), (0,)), ((), ())), preferred_element_type=F32
        )
        st[0, 0] = allow

    def bias_part(i):
        def head(h, carry):
            e = eye(256)
            for t in range(2):
                b = dot_t(e, bias[h, :, 256 * t:256 * t + 256]) * LOG2E
                bt[h, 256 * t:256 * t + 256, :] = jnp.where(st[0, 0, 256 * t:256 * t + 256, :] > 0.5, b, MASKED)
            return carry

        lax.fori_loop(2 * i, 2 * i + 2, head, 0)

    def prep_gate():
        local[2].wait()
        n = xq[:, ka].reshape(S * ROWS, D)
        gate[...] = 1.0 / (1.0 + jnp.exp(-dot(n, wgate[...])))

    def queries(s):
        qs = xq[s].reshape(NQ, D)
        q = (dot_t(wqt[...], qs) * QSCALE).astype(BF)
        for h in range(H):
            off = 64 * (h % 2)
            qtp[s, h, off:off + HD, :] = q[HD * h:HD * h + HD]

    inner = (27.5, 29, 30.5, 32, 34, 35.5, 37, 38.5, 90)

    def window(i, n):
        at = 3 * i + n
        done[0] = int(20 * (inner[at - 1] if at else outer))
        until(inner[at])

    def attend(s):
        ks = xk[s].reshape(NK, D)
        for n in range(4):
            k = dot(ks, wkp[:, 256 * n:256 * n + 256]).astype(BF)
            kp[2 * n] = k[:, :128]
            kp[2 * n + 1] = k[:, 128:]
        for t in range(2):
            v = dot_t(wvt[...], ks[256 * t:256 * t + 256]).astype(BF)
            for h in range(H):
                vt[h, 0:HD, 256 * t:256 * t + 256] = v[HD * h:HD * h + HD]

        def scores(hp):
            tops = []
            for j in range(2):
                h = 2 * hp + j
                top = None
                for c in range(4):
                    v = dot(kp[hp, 128 * c:128 * c + 128, :], qtp[s, h]) + bt[h, 128 * c:128 * c + 128, :]
                    st[hp % 2, j, 128 * c:128 * c + 128, :] = v
                    m = jnp.max(v.reshape(16, 8, NQ), axis=0)
                    top = m if top is None else jnp.maximum(top, m)
                tops.append(jnp.max(top, axis=0, keepdims=True))
            return tops

        def weigh(hp, tops):
            for j in range(2):
                h = 2 * hp + j
                w = jnp.exp2(st[hp % 2, j] - tops[j]).astype(BF)
                o = dot(vt[h], w)
                total = o[HD:HD + 1]
                ot[HD * h:HD * h + HD, :] = (o[:HD] * (1.0 / total)).astype(BF)
                lse[h:h + 1, :] = tops[j] + jnp.log2(total)

        tops = scores(0)
        for hp in range(H // 2):
            if hp in (0, 2, 5):
                for i in range(S - 1):
                    @pl.when(s == i)
                    def _():
                        window(i, (0, 2, 5).index(hp))

            later = scores(hp + 1) if hp < H // 2 - 1 else None
            weigh(hp, tops)
            tops = later
        rest = lse[...]
        for i in range(2):
            part = rest.astype(BF)
            ost[pl.ds(pl.multiple_of(32 * s + 16 * i, 16), 16), :] = part
            rest = rest - part.astype(F32)
        e = eye(256)
        for t in range(3):
            lo = 256 * t
            msg[s, :, :, lo:lo + 256] = dot_t(e, ot[lo:lo + 256, :]).astype(BF).reshape(8, ROWS, 256)
        rbuf[s, ka] = msg[s, ka]

    def rs_send(s, i):
        to = (ka + i) % 8
        return rcopy(msg.at[s, to], rbuf.at[s, ka], rss.at[s, i - 1], rsr.at[s, 8 - i], (pb, to))

    def rs_wait(s, i):
        frm = (ka + i) % 8
        rcopy(msg.at[s, frm], rbuf.at[s, frm], rss.at[s, 0], rsr.at[s, i], (pb, frm)).wait_recv()

    def stat_send(i):
        to = (ka + i) % 8
        return rcopy(smsg.at[to], srbuf.at[ka], sss.at[i - 1], ssr.at[8 - i], (pb, to))

    def stat_wait(i):
        frm = (ka + i) % 8
        rcopy(smsg.at[frm], srbuf.at[frm], sss.at[0], ssr.at[i], (pb, frm)).wait_recv()

    def stats():
        smsg[...] = dot_t(eye(256), ost[...]).astype(BF).reshape(8, ROWS, 128)
        srbuf[ka] = smsg[ka]

    def finish():
        lane = lax.broadcasted_iota(jnp.int32, (128, 128), 1)
        row = lax.broadcasted_iota(jnp.int32, (128, 128), 0)
        erow = lax.broadcasted_iota(jnp.int32, (128, D), 0)
        ecol = lax.broadcasted_iota(jnp.int32, (128, D), 1)
        expand = jnp.logical_and(ecol // HD == erow % 16, erow < 32).astype(F32).astype(BF)
        parts = srbuf[...].reshape(8 * ROWS, 128)
        logs = []
        for s in range(S):
            own = jnp.logical_and(row % 16 == lane % 16, row // 32 == s).astype(F32).astype(BF)
            logs.append(dot(parts, own))
        sums = [jnp.concatenate([v[ROWS * b:ROWS * b + ROWS] for v in logs], axis=0) for b in range(8)]
        top = sums[0]
        for b in range(1, 8):
            top = jnp.maximum(top, sums[b])
        w = [jnp.exp2(v - top) for v in sums]
        total = w[0]
        for b in range(1, 8):
            total = total + w[b]
        inv = 1.0 / total
        acc = jnp.zeros((S * ROWS, D), F32)
        for b in range(8):
            v = w[b] * inv
            hi = v.astype(BF)
            low = (v - hi.astype(F32)).astype(BF)
            both = jnp.where(lane < 16, hi.astype(F32), jnp.where(lane < 32, low.astype(F32), 0.0)).astype(BF)
            acc = acc + dot(both, expand) * rbuf[:, b].reshape(S * ROWS, D).astype(F32)
        gated = (gate[...] * acc).astype(BF)
        local[3].wait()
        mixed = act[...].reshape(S * ROWS, D).astype(F32) + dot(gated, wout[...])
        normed = norm(mixed, gain2[...].reshape(1, D)).astype(BF)
        local[4].wait()
        left = dot(normed, wup[:, :FF])
        right = dot(normed, wup[:, FF:])
        hidden = (left / (1.0 + jnp.exp(-left)) * right).astype(BF)
        local[5].wait()
        out[...] = (mixed + dot(hidden, wdown[...])).astype(BF).reshape(S, ROWS, D)

    until(1)
    turn_query_weights()
    until(3.4)
    turn_value_weights()
    until(4)
    pad_key_weights()
    until(5)
    prep_bias()
    until(6)
    for i in range(8):
        bias_part(i)
        until(7 + i)
    queries(0)
    until(15)
    prep_gate()
    until(16)
    queries(1)
    for us in (17, 18, 19, 20):
        until(us)
    queries(2)
    for us in (21, 22, 23):
        until(us)
    outer = 25.5
    until(outer)
    queries(3)

    def step(s, carry):
        twin_recv(s)
        attend(s)
        for i in (4, 3, 5, 2, 6, 1, 7):
            rs_send(s, i).start()
        return carry

    def twin_recv(s):
        rcopy(xk.at[s, 1 - core], xk.at[s, 1 - core], ds.at[s], dr.at[s], (twin, ka)).wait_recv()

    lax.fori_loop(0, S, step, 0)

    stats()
    for i in (4, 3, 5, 2, 6, 1, 7):
        stat_send(i).start()
    for s in range(S):
        for i in range(1, 8):
            rs_wait(s, i)
    for i in range(1, 8):
        stat_wait(i)
    finish()

    for s in range(S):
        for i in range(1, 8):
            rs_send(s, i).wait_send()
        twin_send(s, xq.at[s]).wait_send()
    for i in range(1, 8):
        stat_send(i).wait_send()

    def settle(c):
        for at, ev in plans[c]:
            if ev[0] == "send":
                sent(c, *ev[1:]).wait_send()

    each_class(settle)


def body(act, gain1, wqkv, wgate, wout, bias, chain, binder, gain2, wup, wdown):
    vmem = pl.BlockSpec(memory_space=pltpu.VMEM)
    hbm = pl.BlockSpec(memory_space=pl.ANY)
    dma, v = pltpu.SemaphoreType.DMA, pltpu.VMEM
    return pl.pallas_call(
        kernel,
        out_shape=jax.ShapeDtypeStruct((S, ROWS, D), BF),
        in_specs=[vmem, vmem, hbm, hbm, hbm, hbm, vmem, vmem, vmem, hbm, hbm],
        out_specs=vmem,
        scratch_shapes=[
            v((S, 8, ROWS, D), BF), v((S, 2, 8, ROWS, D), BF), v((S, 2, ROWS, D), BF),
            v((D, 3 * D), BF), v((D, D), BF), v((D, D), BF), v((D, 2 * FF), BF), v((FF, D), BF),
            v((H, NQ, NK), BF), v((H, NK, NQ), F32),
            v((D, D), BF), v((D, D), BF), v((D, 1024), BF),
            v((S, H, 128, NQ), BF), v((H // 2, NK, 128), BF), v((H, 64, NK), BF),
            v((2, 2, NK, NQ), F32), v((D, NQ), BF), v((H, NQ), F32),
            v((S, 8, ROWS, D), BF), v((S, 8, ROWS, D), BF),
            v((8, ROWS, 128), BF), v((8, ROWS, 128), BF), v((128, NQ), BF), v((S * ROWS, D), F32),
            dma((6,)), dma((S, 7)), dma((S, 4, 2)), dma((S, 8)), dma((S, 8)), dma((S, 4)),
            dma((S, 2)), dma((S, 2)), dma((S,)), dma((S,)), dma((S, 7)), dma((S, 8)),
            dma((7,)), dma((8,)),
        ],
        compiler_params=pltpu.CompilerParams(
            collective_id=0, has_side_effects=True, vmem_limit_bytes=66_000_000
        ),
        name="block",
    )(
        act, gain1, wqkv, wgate, wout, bias, chain.reshape(32, 128), binder.reshape(32, 128),
        gain2, wup, wdown,
    )


def solution(mesh):
    placed = (
        P(None, ("pb", "ka"), None), P(), P(), P(), P(), P(None, "pb", "ka"), P(), P(), P(), P(), P(),
    )
    return jax.shard_map(
        body, mesh=mesh, in_specs=placed, out_specs=P(None, ("pb", "ka"), None), check_vma=False
    )
```

time: 206 us -> 73 us (0.35)
  the two profiles are of different devices: /device:TPU:120 before, /device:TPU:1 now
where the time goes in v3:
time: 73 us; the launch traced here: 72.8 us
  Pallas kernels  71.2 us (98%)
  local copies, waits for them, and re-layouts  1.62 us (2%)
    pallas_call x1, Pallas kernels, body(): pl.pallas_call(kernel, out_shape=jax.ShapeDtypeStruct((S, ROWS, D), BF),...  71.2 us
    unnamed x1, local copies, waits for them, and re-layouts  1.62 us

profile of v3, /device:TPU:1, one launch (start us, length us, event | category | flops | bytes accessed | tf_op | source)
XLA Modules:
  0.0 72.8 jit_solution(1969879484094213967)
XLA Ops:
  0.0 71.2 %block.1 = bf16[4,32,768]{2,1,0:T(8,128)(2,1)} custom-call(bf16[4,32,768]{2,1,0:T(8,128)(2,1)} %act.1, f32[768]{0:T(1024)} %gain1.1, bf16[768,2304]{1,0:T(8,128)(2,1)} %wqkv_h.1, bf16[768,768]{1,0:T(8,128)(2,1)} %wgate_h.1, bf16[768,768]{1,0:T(8,128)(2,1)} %wout_h.1, bf16[16,256,512]{2,1,0:T(8,128)(2,1)} %bias_h.1, s32[32,128]{1,0:T(8,128)} %bitcast.2, ...), custom_call_target="tpu_custom_call" | custom-call | tf_op jit(solution)/shard_map/block/pallas_call | solution.py:518
  71.2 1.6 %copy.13 = bf16[4,32,768]{2,1,0:T(8,128)(2,1)} copy(bf16[4,32,768]{2,1,0:T(8,128)(2,1)} %block.1) | data formatting | bytes 393216

commit v4 on v3

--- a/solution.py
+++ b/solution.py
@@ -39,6 +39,8 @@
 
 UP = ((0, 0), (1, 0), (1, 1), (2, 0))
 DOWN = ((0, 1), (3, 0), (3, 1), (2, 1))
+ROUND = ((0, 0), (0, 1), (1, 0), (3, 0))
+DIRECT = ((1, 0), (3, 0), (2, 0), (2, 1))
 CLASSES = [(e, r) for e in (1, 0) for r in range(4)]
 
 
@@ -50,10 +52,10 @@
     s, kind = op[1], op[0]
     if kind in ("own", "mate", "far", "relay"):
         return s + ("own", "mate", "far", "relay").index(kind)
-    return 10 * s + (op[3] if kind == "z" else op[2])
-
-
-def traffic(occupied=23, latency=44):
+    return 10 * s + (op[3] if kind == "z" else (ROUND if kind == "side" else DIRECT).index(op[2:]))
+
+
+def traffic(occupied=22, latency=56):
     have = {c: {} for c in CLASSES}
     pend, free, log = {}, {}, {c: [] for c in CLASSES}
     for c in CLASSES:
@@ -72,11 +74,10 @@
                     if r != end:
                         ops[d].append((("z", s, d, g), ("q" if c == (1, 0) else "k", s) + owners[g]))
             if c == (0, 0):
-                ops["o"] += [(("cross", s, dx, dy), ("q", s, dx, dy)) for dx in (0, 2) for dy in (0, 1)]
-            if e == 0 and r in (1, 3):
-                for dy in (0, 1):
-                    ops["o"].append((("side", s, dy), ("q", s, 0, dy)))
-                    ops["x+" if r == 1 else "x-"].append((("relay", s, dy), ("rl", s, dy)))
+                ops["o"] += [(("cross", s) + o, ("q", s) + o) for o in DIRECT]
+            if c == (1, 0):
+                ops["o"] += [(("side", s) + o, ("q", s) + o) for o in ROUND]
+                ops["y"] += [(("relay", s) + o, ("rl", s) + o) for o in ROUND]
         pend[c] = ops
         free.update({(c, l): 0 for l in ops})
     for now in range(2000):
@@ -100,7 +101,7 @@
                 elif op[0] == "side":
                     item = ("rl",) + op[1:]
                 elif op[0] == "relay":
-                    item = ("k", s, 3 if r == 1 else 1, op[2])
+                    item = ("k", s, op[2], 1 - op[3])
                 elif l == "y":
                     item = ("q", s, 0, 1)
                 elif op[0] == "far":
@@ -169,9 +170,7 @@
             ((wqkv_h, wqkv), (bias_h, bias), (wgate_h, wgate), (wout_h, wout), (wup_h, wup), (wdown_h, wdown))
         )
     ]
-    for c in local:
-        c.start()
-
+    local[0].start()
     barrier = pltpu.get_barrier_semaphore()
     for i in range(1, 8):
         pl.semaphore_signal(barrier, inc=1, device_id=(pb, (ka + i) % 8), device_id_type=MESH)
@@ -180,8 +179,6 @@
 
     for s in range(S):
         xq[s, ka] = norm(act[s].astype(F32), gain1[...].reshape(1, D)).astype(BF)
-
-    pl.semaphore_wait(barrier, 11)
 
     def q_at(dx, dy):
         return ((x + dx) % 4) * 2 + (ylo + dy) % 2
@@ -210,14 +207,15 @@
             n = slot(*owner)
             src = xq if item[0] == "q" else xk.at[:, core]
             return rcopy(src.at[s, at], xk.at[s, core, at], zs.at[s, n], zr.at[s, n], (zp if link == "z+" else zm, ka))
+        owner, at = item[2:], q_at(*item[2:])
         if kind == "cross":
-            at = q_at(*item[2:])
-            return rcopy(xq.at[s, at], xk.at[s, core, at], crs.at[s, op[2] + op[3]], zr.at[s, slot(*item[2:])], opp)
-        dy = op[2]
+            n = DIRECT.index(owner)
+            return rcopy(xq.at[s, at], xk.at[s, core, at], crs.at[s, n], zr.at[s, slot(*owner)], opp)
+        n = ROUND.index(owner)
         if kind == "side":
-            return rcopy(xq.at[s, q_at(0, dy)], rl.at[s, dy], crs.at[s, dy], rlr.at[s, dy], opp)
-        n = slot(3 if c[1] == 1 else 1, dy)
-        return rcopy(rl.at[s, dy], xk.at[s, core, k_at(0, dy)], rls.at[s, dy], zr.at[s, n], (pb, xp if c[1] == 1 else xm))
+            return rcopy(xq.at[s, at], rl.at[s, n], crs.at[s, n], rlr.at[s, n], opp)
+        dx, dy = owner
+        return rcopy(rl.at[s, n], xk.at[s, core, q_at(dx, 1 - dy)], rls.at[s, n], zr.at[s, slot(dx, 1 - dy)], (pb, mate))
 
     def arrived(item):
         s = item[1]
@@ -227,7 +225,8 @@
             n = slot(*item[2:])
             ref, ssem, rsem = xk.at[s, core, k_at(*item[2:])], zs.at[s, n], zr.at[s, n]
         else:
-            ref, ssem, rsem = rl.at[s, item[2]], rls.at[s, item[2]], rlr.at[s, item[2]]
+            n = ROUND.index(item[2:])
+            ref, ssem, rsem = rl.at[s, n], rls.at[s, n], rlr.at[s, n]
         rcopy(ref, ref, ssem, rsem, opp).wait_recv()
 
     def twin_send(s, src):
@@ -244,7 +243,7 @@
     done = [0]
 
     def until(us):
-        low, high = done[0], int(us * 20)
+        low, high = done[0], round(20 * us)
         done[0] = high
         for c in CLASSES:
             events = [ev for at, ev in plans[c] if low <= at < high]
@@ -328,11 +327,14 @@
             off = 64 * (h % 2)
             qtp[s, h, off:off + HD, :] = q[HD * h:HD * h + HD]
 
-    inner = (27.5, 29, 30.5, 32, 34, 35.5, 37, 38.5, 90)
+    ready = [max(at for p in plans.values() for at, ev in p if ev == ("twin", s)) / 20 + 0.05 for s in range(S)]
+    outer = ready[0]
+    inner = [ready[i] + (ready[i + 1] - ready[i]) * (n + 1) / 3 for i in range(S - 1) for n in range(3)]
+    inner[-1] = 90
 
     def window(i, n):
         at = 3 * i + n
-        done[0] = int(20 * (inner[at - 1] if at else outer))
+        done[0] = round(20 * (inner[at - 1] if at else outer))
         until(inner[at])
 
     def attend(s):
@@ -448,8 +450,12 @@
         local[5].wait()
         out[...] = (mixed + dot(hidden, wdown[...])).astype(BF).reshape(S, ROWS, D)
 
+    local[1].start()
+    pl.semaphore_wait(barrier, 11)
     until(1)
     turn_query_weights()
+    for c in local[2:]:
+        c.start()
     until(3.4)
     turn_value_weights()
     until(4)
@@ -470,9 +476,10 @@
     queries(2)
     for us in (21, 22, 23):
         until(us)
-    outer = 25.5
+    until(24)
+    queries(3)
+    until(25)
     until(outer)
-    queries(3)
 
     def step(s, carry):
         twin_recv(s)
@@ -521,7 +528,7 @@
         in_specs=[vmem, vmem, hbm, hbm, hbm, hbm, vmem, vmem, vmem, hbm, hbm],
         out_specs=vmem,
         scratch_shapes=[
-            v((S, 8, ROWS, D), BF), v((S, 2, 8, ROWS, D), BF), v((S, 2, ROWS, D), BF),
+            v((S, 8, ROWS, D), BF), v((S, 2, 8, ROWS, D), BF), v((S, 4, ROWS, D), BF),
             v((D, 3 * D), BF), v((D, D), BF), v((D, D), BF), v((D, 2 * FF), BF), v((FF, D), BF),
             v((H, NQ, NK), BF), v((H, NK, NQ), F32),
             v((D, D), BF), v((D, D), BF), v((D, 1024), BF),
@@ -530,7 +537,7 @@
             v((S, 8, ROWS, D), BF), v((S, 8, ROWS, D), BF),
             v((8, ROWS, 128), BF), v((8, ROWS, 128), BF), v((128, NQ), BF), v((S * ROWS, D), F32),
             dma((6,)), dma((S, 7)), dma((S, 4, 2)), dma((S, 8)), dma((S, 8)), dma((S, 4)),
-            dma((S, 2)), dma((S, 2)), dma((S,)), dma((S,)), dma((S, 7)), dma((S, 8)),
+            dma((S, 4)), dma((S, 4)), dma((S,)), dma((S,)), dma((S, 7)), dma((S, 8)),
             dma((7,)), dma((8,)),
         ],
         compiler_params=pltpu.CompilerParams(

time: 73 us -> 71.2 us (0.975)
  Pallas kernels: 71.2 us -> 69.4 us
    pallas_call x1, Pallas kernels: 71.2 us -> 69.4 us  [body(): pl.pallas_call(kernel, out_shape=jax.ShapeDtypeStruct((S, ROWS, D), BF),...]
where the time goes in v4:
time: 71.2 us; the launch traced here: 71 us
  Pallas kernels  69.4 us (97%)
  local copies, waits for them, and re-layouts  1.62 us (2%)
    pallas_call x1, Pallas kernels, body(): pl.pallas_call(kernel, out_shape=jax.ShapeDtypeStruct((S, ROWS, D), BF),...  69.4 us
    unnamed x1, local copies, waits for them, and re-layouts  1.62 us

profile of v4, /device:TPU:1, one launch (start us, length us, event | category | flops | bytes accessed | tf_op | source)
XLA Modules:
  0.0 71.0 jit_solution(5393984849520333094)
XLA Ops:
  0.0 69.4 %block.1 = bf16[4,32,768]{2,1,0:T(8,128)(2,1)} custom-call(bf16[4,32,768]{2,1,0:T(8,128)(2,1)} %act.1, f32[768]{0:T(1024)} %gain1.1, bf16[768,2304]{1,0:T(8,128)(2,1)} %wqkv_h.1, bf16[768,768]{1,0:T(8,128)(2,1)} %wgate_h.1, bf16[768,768]{1,0:T(8,128)(2,1)} %wout_h.1, bf16[16,256,512]{2,1,0:T(8,128)(2,1)} %bias_h.1, s32[32,128]{1,0:T(8,128)} %bitcast.2, ...), custom_call_target="tpu_custom_call" | custom-call | tf_op jit(solution)/shard_map/block/pallas_call | solution.py:525
  69.4 1.6 %copy.13 = bf16[4,32,768]{2,1,0:T(8,128)(2,1)} copy(bf16[4,32,768]{2,1,0:T(8,128)(2,1)} %block.1) | data formatting | bytes 393216

commit v5 on v4

--- a/solution.py
+++ b/solution.py
@@ -329,11 +329,11 @@
 
     ready = [max(at for p in plans.values() for at, ev in p if ev == ("twin", s)) / 20 + 0.05 for s in range(S)]
     outer = ready[0]
-    inner = [ready[i] + (ready[i + 1] - ready[i]) * (n + 1) / 3 for i in range(S - 1) for n in range(3)]
+    inner = [ready[i] + (ready[i + 1] - ready[i]) * (n + 1) / 2 for i in range(S - 1) for n in range(2)]
     inner[-1] = 90
 
     def window(i, n):
-        at = 3 * i + n
+        at = 2 * i + n
         done[0] = round(20 * (inner[at - 1] if at else outer))
         until(inner[at])
 
@@ -372,11 +372,11 @@
 
         tops = scores(0)
         for hp in range(H // 2):
-            if hp in (0, 2, 5):
+            if hp in (0, 4):
                 for i in range(S - 1):
                     @pl.when(s == i)
                     def _():
-                        window(i, (0, 2, 5).index(hp))
+                        window(i, (0, 4).index(hp))
 
             later = scores(hp + 1) if hp < H // 2 - 1 else None
             weigh(hp, tops)

time: 71.2 us -> 70.6 us (level)
  no operation moved by 1% of the time
where the time goes in v5:
time: 70.6 us; the launch traced here: 70.4 us
  Pallas kernels  68.8 us (97%)
  local copies, waits for them, and re-layouts  1.62 us (2%)
    pallas_call x1, Pallas kernels, body(): pl.pallas_call(kernel, out_shape=jax.ShapeDtypeStruct((S, ROWS, D), BF),...  68.8 us
    unnamed x1, local copies, waits for them, and re-layouts  1.62 us

profile of v5, /device:TPU:1, one launch (start us, length us, event | category | flops | bytes accessed | tf_op | source)
XLA Modules:
  0.0 70.4 jit_solution(8120882808607108474)
XLA Ops:
  0.0 68.8 %block.1 = bf16[4,32,768]{2,1,0:T(8,128)(2,1)} custom-call(bf16[4,32,768]{2,1,0:T(8,128)(2,1)} %act.1, f32[768]{0:T(1024)} %gain1.1, bf16[768,2304]{1,0:T(8,128)(2,1)} %wqkv_h.1, bf16[768,768]{1,0:T(8,128)(2,1)} %wgate_h.1, bf16[768,768]{1,0:T(8,128)(2,1)} %wout_h.1, bf16[16,256,512]{2,1,0:T(8,128)(2,1)} %bias_h.1, s32[32,128]{1,0:T(8,128)} %bitcast.2, ...), custom_call_target="tpu_custom_call" | custom-call | tf_op jit(solution)/shard_map/block/pallas_call | solution.py:525
  68.8 1.6 %copy.13 = bf16[4,32,768]{2,1,0:T(8,128)(2,1)} copy(bf16[4,32,768]{2,1,0:T(8,128)(2,1)} %block.1) | data formatting | bytes 393216
